TPU v7x, 32 devices: a whole 2x2x4 slice. The times are simulated.
32 devices in a mesh: band: 4 (over x, core), grid: 8 (over z, y).
Axes of the slice: x: 2, y: 2, z: 4, core: 2. Of those that a mesh axis runs over, the one named last changes fastest.
Arguments:
- orbitals: float32 [8, 128, 128, 128], P('band', 'grid'), may hold values from -6 to 6
- occupation: float32 [8], P('band'), may hold values from 0.25 to 1
- g_list: int32 [131072], P('grid'), may hold values from 0 to 262143, as said below
- positions: float32 [3, 512], replicated, may hold values from 0 to 1
- species: int32 [512], replicated, may hold values from 0 to 3
- widths: float32 [4], replicated, may hold values from 0.3 to 2
Outputs:
- stress: float32 [3, 3], replicated
- atom_terms: float32 [512], replicated
Inputs may be any that keep to these rules, and one draw needn't show every extreme that they name: `g_list`: within each aligned block of 16384 entries the values are distinct and increasing.
All inputs are finite; a program needn't handle non-finite values.
Results may differ from a plain program's by a relative error of at most 0.00013.
Values sent between devices are 32-bit elements; how exact they have to be, the bound alone decides.
No kernel may reach another device: no remote copies, remote signals or barrier semaphores. Data moves between devices by JAX's collectives and lax.ppermute only.
A program may use at most 64 MiB of HBM per device.

v0:
```python
import math
import jax
import jax.numpy as jnp
from jax import lax
from jax.sharding import PartitionSpec as P

HIGHEST = lax.Precision.HIGHEST


def shifted(array, axis, by):
    peers = lax.axis_size(axis)
    return lax.ppermute(array, axis, [(i, (i + by) % peers) for i in range(peers)])


def dft_tables(length):
    indices = jnp.arange(length, dtype=jnp.int32)
    products = indices[:, None] * indices[None, :] % length
    angles = 2.0 * math.pi / length * products.astype(jnp.float32)
    return (jnp.cos(angles), jnp.sin(angles))


def folded_frequency(cell, length):
    folded = jnp.where(cell < length // 2, cell, cell - length)
    return folded.astype(jnp.float32)


def spectrum_sums(
    selected, freq_x, freq_y, freq_z, positions, species, widths, lengths, band_total
):
    two_pi = 2.0 * math.pi
    wave_vector = jnp.stack(
        [two_pi * freq_x / lengths[0], two_pi * freq_y / lengths[1], two_pi * freq_z / lengths[2]]
    )
    wave_square = jnp.sum(wave_vector * wave_vector, axis=0)
    nonzero = (wave_square > 0).astype(jnp.float32)
    denominator = wave_square + 1.0 - nonzero
    weighted = selected * (4.0 * math.pi) * nonzero / denominator
    identity = jnp.eye(3, dtype=jnp.float32)[:, :, None]
    kernel = 2.0 * wave_vector[:, None, :] * wave_vector[None, :, :] / denominator - identity
    stress = jnp.sum(kernel * weighted[None, None, :], axis=2) / band_total
    form_factor = (
        jnp.exp(-0.5 * wave_square[None, :] * (widths * widths)[:, None]) * weighted[None, :]
    )
    kinds = widths.shape[0]
    one_hot = (species[:, None] == jnp.arange(kinds, dtype=jnp.int32)[None, :]).astype(jnp.float32)
    atom_count = species.shape[0]
    fractions = positions.reshape(3, atom_count // 32, 32).transpose(1, 0, 2)
    hot_rows = one_hot.reshape(atom_count // 32, 32, kinds)

    def atom_block(operands):
        fraction, hot_block = operands
        phases = two_pi * (
            fraction[0][:, None] * freq_x[None, :]
            + fraction[1][:, None] * freq_y[None, :]
            + fraction[2][:, None] * freq_z[None, :]
        )
        projected = jnp.dot(jnp.cos(phases), form_factor.T, precision=HIGHEST)
        return jnp.sum(projected * hot_block, axis=1)

    atom_terms = lax.map(atom_block, (fractions, hot_rows)).reshape(atom_count) / band_total
    return (stress, atom_terms)


def per_device(orbitals, occupation, g_list, positions, species, widths):
    block_bands, slab_x, size_y, size_z = orbitals.shape
    grid_count = lax.axis_size("grid")
    band_count = lax.axis_size("band")
    size_x = slab_x * grid_count
    slab_y = size_y // grid_count
    cells = size_x * size_y * size_z
    scale = 1.0 / (float(cells) * float(cells))
    cos_x, sin_x = dft_tables(size_x)
    cos_y, sin_y = dft_tables(size_y)
    cos_z, sin_z = dft_tables(size_z)

    def finish_x(exchanged):
        real_part = exchanged[:, 0]
        imag_part = exchanged[:, 1]
        real_x = jnp.einsum("pxyz,mx->pmyz", real_part, cos_x, precision=HIGHEST) + jnp.einsum(
            "pxyz,mx->pmyz", imag_part, sin_x, precision=HIGHEST
        )
        imag_x = jnp.einsum("pxyz,mx->pmyz", imag_part, cos_x, precision=HIGHEST) - jnp.einsum(
            "pxyz,mx->pmyz", real_part, sin_x, precision=HIGHEST
        )
        return real_x * real_x + imag_x * imag_x

    def add_pairs(accumulated, right_rows, right_occupied, factor):

        def one_band(band_index, running):
            orbital_row = lax.dynamic_index_in_dim(orbitals, band_index, 0, keepdims=False)
            occupied = lax.dynamic_index_in_dim(occupation, band_index, 0, keepdims=False)
            pair_rows = orbital_row[None] * right_rows
            weights = occupied * right_occupied * (factor * scale)
            real_z = jnp.einsum("pxyz,kz->pxyk", pair_rows, cos_z, precision=HIGHEST)
            imag_z = -jnp.einsum("pxyz,kz->pxyk", pair_rows, sin_z, precision=HIGHEST)
            real_y = jnp.einsum("pxyk,my->pxmk", real_z, cos_y, precision=HIGHEST) + jnp.einsum(
                "pxyk,my->pxmk", imag_z, sin_y, precision=HIGHEST
            )
            imag_y = jnp.einsum("pxyk,my->pxmk", imag_z, cos_y, precision=HIGHEST) - jnp.einsum(
                "pxyk,my->pxmk", real_z, sin_y, precision=HIGHEST
            )
            stacked = jnp.stack([real_y, imag_y], axis=1)
            pair_power = finish_x(
                lax.all_to_all(stacked, "grid", split_axis=3, concat_axis=2, tiled=True)
            )
            return running + jnp.einsum("p,pxyz->xyz", weights, pair_power, precision=HIGHEST)

        return lax.fori_loop(0, block_bands, one_band, accumulated)

    empty = jnp.zeros((size_x, slab_y, size_z), jnp.float32)
    spectrum = add_pairs(empty, orbitals, occupation, 1.0)
    for distance in range(1, band_count // 2 + 1):
        neighbour = shifted((orbitals, occupation), "band", distance)
        factor = 2.0 if 2 * distance < band_count else 1.0
        spectrum = add_pairs(spectrum, neighbour[0], neighbour[1], factor)
    flat_spectrum = spectrum.reshape(-1)
    selected = jnp.take(flat_spectrum, g_list)
    cell_x = g_list // (slab_y * size_z)
    cell_y = lax.axis_index("grid") * slab_y + g_list // size_z % slab_y
    cell_z = g_list % size_z
    stress, atom_terms = spectrum_sums(
        selected,
        folded_frequency(cell_x, size_x),
        folded_frequency(cell_y, size_y),
        folded_frequency(cell_z, size_z),
        positions,
        species,
        widths,
        (size_x, size_y, size_z),
        block_bands * band_count,
    )
    stress, atom_terms = lax.psum((stress, atom_terms), ("band", "grid"))
    return (stress, atom_terms)


def solution(mesh):
    return jax.shard_map(
        per_device,
        mesh=mesh,
        in_specs=(P("band", "grid", None, None), P("band"), P("grid"), P(), P(), P()),
        out_specs=(P(), P()),
        check_vma=False,
    )
```

profile of v0, /device:TPU:12, one launch (start us, length us, event | category | flops | bytes accessed | tf_op | source)
XLA Modules:
  0.0 1331.4 jit_solution(5733320906474539223)
XLA Ops:
  13.5 339.4 %while.62 = (s32[]{:T(128)}, f32[128,16,128]{2,1,0:T(8,128)S(1)}, f32[2]{0:T(128)}, f32[2,16,128,128]{3,2,1,0:T(8,128)}, s32[]{:T(128)}, /*index=5*/s32[]{:T(128)}) while((s32[]{:T(128)}, f32[128,16,128]{2,1,0:T(8,128)S(1)}, f32[2]{0:T(128)}, f32[2,16,128,128]{3,2,1,0:T(8,128)}, s32[]{:T(128)}, ...), condition=%wide.region_2.3_spmd.clone.clone, body=%wide.region_1.2_spmd.clone.clone.sunk | while | flops 8068988928 | bytes 146800944 | solution.py:108
  46.4 89.6 %all-to-all-done.2 = f32[2,2,16,128,128]{4,2,0,1,3:T(8,128)} async-done(((f32[2,2,16,128,128]{4,2,0,1,3:T(8,128)}), f32[2,2,16,128,128]{4,2,0,1,3:T(8,128)}, u32[]{:S(2)}, u32[]{:S(2)}) %all-to-all-start.2) | async-done | bytes 4194336 | tf_op jit(solution)/shard_map/while/body/eval_jaxpr/all_to_all | solution.py:104
  206.0 88.7 %all-to-all-done.2 = f32[2,2,16,128,128]{4,2,0,1,3:T(8,128)} async-done(((f32[2,2,16,128,128]{4,2,0,1,3:T(8,128)}), f32[2,2,16,128,128]{4,2,0,1,3:T(8,128)}, u32[]{:S(2)}, u32[]{:S(2)}) %all-to-all-start.2) | async-done | bytes 4194336 | tf_op jit(solution)/shard_map/while/body/eval_jaxpr/all_to_all | solution.py:104
  352.9 323.8 %while.60 = (s32[]{:T(128)}, f32[128,16,128]{2,1,0:T(8,128)S(1)}, f32[2]{0:T(128)}, f32[2]{0:T(128)}, f32[2,16,128,128]{3,2,1,0:T(8,128)}, /*index=5*/f32[2,16,128,128]{3,2,1,0:T(8,128)}, s32[]{:T(128)}) while((s32[]{:T(128)}, f32[128,16,128]{2,1,0:T(8,128)S(1)}, f32[2]{0:T(128)}, f32[2]{0:T(128)}, ...), condition=%wide.region_4.5_spmd.clone.clone, body=%wide.region_3.4_spmd.clone.clone.sunk | while | flops 8068726784 | bytes 138412304 | solution.py:108
  390.0 88.6 %all-to-all-done = f32[2,2,16,128,128]{4,2,0,1,3:T(8,128)} async-done(((f32[2,2,16,128,128]{4,2,0,1,3:T(8,128)}), f32[2,2,16,128,128]{4,2,0,1,3:T(8,128)}, u32[]{:S(2)}, u32[]{:S(2)}) %all-to-all-start) | async-done | bytes 4194336 | tf_op jit(solution)/shard_map/while/body/eval_jaxpr/all_to_all | solution.py:104
  505.7 8.9 fusion.492
  551.9 88.6 %all-to-all-done = f32[2,2,16,128,128]{4,2,0,1,3:T(8,128)} async-done(((f32[2,2,16,128,128]{4,2,0,1,3:T(8,128)}), f32[2,2,16,128,128]{4,2,0,1,3:T(8,128)}, u32[]{:S(2)}, u32[]{:S(2)}) %all-to-all-start) | async-done | bytes 4194336 | tf_op jit(solution)/shard_map/while/body/eval_jaxpr/all_to_all | solution.py:104
  667.6 8.9 fusion.492
  676.8 354.2 %while.61 = (s32[]{:T(128)}, f32[128,16,128]{2,1,0:T(8,128)S(1)}, f32[2]{0:T(128)}, f32[2]{0:T(128)}, f32[2,16,128,128]{3,2,1,0:T(8,128)}, /*index=5*/f32[2,16,128,128]{3,2,1,0:T(8,128)}, s32[]{:T(128)}) while((s32[]{:T(128)}, f32[128,16,128]{2,1,0:T(8,128)S(1)}, f32[2]{0:T(128)}, f32[2]{0:T(128)}, ...), condition=%wide.region_6.7_spmd.clone.clone, body=%wide.region_5.6_spmd.clone.clone.sunk | while | flops 8068726784 | bytes 138412304 | solution.py:108
  736.4 88.7 %all-to-all-done.1 = f32[2,2,16,128,128]{4,2,0,1,3:T(8,128)} async-done(((f32[2,2,16,128,128]{4,2,0,1,3:T(8,128)}), f32[2,2,16,128,128]{4,2,0,1,3:T(8,128)}, u32[]{:S(2)}, u32[]{:S(2)}) %all-to-all-start.1) | async-done | bytes 4194336 | tf_op jit(solution)/shard_map/while/body/eval_jaxpr/all_to_all | solution.py:104
  852.1 8.9 fusion.522
  898.3 88.7 %all-to-all-done.1 = f32[2,2,16,128,128]{4,2,0,1,3:T(8,128)} async-done(((f32[2,2,16,128,128]{4,2,0,1,3:T(8,128)}), f32[2,2,16,128,128]{4,2,0,1,3:T(8,128)}, u32[]{:S(2)}, u32[]{:S(2)}) %all-to-all-start.1) | async-done | bytes 4194336 | tf_op jit(solution)/shard_map/while/body/eval_jaxpr/all_to_all | solution.py:104
  1014.0 8.9 fusion.522
  1031.1 90.5 %gather_fusion = f32[16384]{0:T(1024)S(1)} fusion(f32[262144]{0:T(1024)S(1)} %bitcast.377, s32[16384]{0:T(1024)S(1)} %copy-done.11), kind=kCustom, calls=%fused_computation | custom fusion | bytes 196608 | tf_op jit(solution)/shard_map/jit(_take)/gather | solution.py:117
  1122.3 166.4 %while.59 = (s32[]{:T(128)}, f32[16,32]{1,0:T(8,128)S(1)}, f32[16,3,32]{2,0,1:T(8,128)}, f32[16384]{0:T(1024)S(1)}, f32[16384]{0:T(1024)S(1)}, /*index=5*/f32[16...) while((s32[]{:T(128)}, f32[16,32]{1,0:T(8,128)S(1)}, ...), condition=%wide.region_11.12_spmd.clone, body=%wide.region_9.11_spmd.clone.sunk | while | flops 28442852 | bytes 329921 | solution.py:60
  1123.0 9.6 fusion.462
  1133.4 9.6 fusion.462
  1143.8 9.6 fusion.462
  1154.2 9.6 fusion.462
  1164.6 9.6 fusion.462
  1175.0 9.6 fusion.462
  1185.4 9.6 fusion.462
  1195.8 9.7 fusion.462
  1206.2 9.6 fusion.462
  1216.6 9.7 fusion.462
  1227.1 9.6 fusion.462
  1237.5 9.7 fusion.462
  1247.9 9.6 fusion.462
  1258.3 9.6 fusion.462
  1268.7 9.6 fusion.462
  1279.1 9.6 fusion.462
  1288.8 42.1 %all-reduce = (f32[3,3]{1,0:T(4,128)}, f32[512]{0:T(512)}) all-reduce(f32[3,3]{1,0:T(4,128)S(1)} %broadcast_multiply_fusion.6, f32[512]{0:T(512)S(1)} %div.77), channel_id=1, replica_groups=mesh['band'=4,'grid'=8] {'band','grid'}, use_global_device_ids=true, to_apply=%region_8.9 | all-reduce | flops 521 | bytes 4168 | tf_op jit(solution)/shard_map/psum | solution.py:132
  (245 shorter events, 420.6 us)
Async XLA Ops:
  0.6 352.2 %collective-permute-start.1 = (f32[2,16,128,128]{3,2,1,0:T(8,128)}, f32[2,16,128,128]{3,2,1,0:T(8,128)}, u32[]{:S(2)}, u32[]{:S(2)}) collective-permute-start(f32[2,16,128,128]{3,2,1,0:T(8,128)} %param.14), channel_id=1, source_target_pairs={{0,8},{8,16},{16,24},{24,0},{1,9},{9,17},{17,25},{25,1},{2,10},{10... | collective-permute-start | bytes 6291464 | tf_op jit(solution)/shard_map/ppermute | solution.py:12
  0.7 676.0 %collective-permute-start.3 = (f32[2,16,128,128]{3,2,1,0:T(8,128)}, f32[2,16,128,128]{3,2,1,0:T(8,128)}, u32[]{:S(2)}, u32[]{:S(2)}) collective-permute-start(f32[2,16,128,128]{3,2,1,0:T(8,128)} %param.14), channel_id=1, source_target_pairs={{0,16},{8,24},{16,0},{24,8},{1,17},{9,25},{17,1},{25,9},{2,18},{10... | collective-permute-start | bytes 6291464 | tf_op jit(solution)/shard_map/ppermute | solution.py:12
  2.3 350.6 %collective-permute-start = (f32[2]{0:T(128)}, f32[2]{0:T(128)}, u32[]{:S(2)}, u32[]{:S(2)}) collective-permute-start(f32[2]{0:T(128)} %param.15), channel_id=1, source_target_pairs={{0,8},{8,16},{16,24},{24,0},{1,9},{9,17},{17,25},{25,1},{2,10},{10... | collective-permute-start | bytes 32 | tf_op jit(solution)/shard_map/ppermute | solution.py:12
  2.5 350.3 %collective-permute-start.2 = (f32[2]{0:T(128)}, f32[2]{0:T(128)}, u32[]{:S(2)}, u32[]{:S(2)}) collective-permute-start(f32[2]{0:T(128)} %param.15), channel_id=1, source_target_pairs={{0,16},{8,24},{16,0},{24,8},{1,17},{9,25},{17,1},{25,9},{2,18},{10... | collective-permute-start | bytes 32 | tf_op jit(solution)/shard_map/ppermute | solution.py:12
  39.4 6.4 copy-start.17
  39.4 96.5 %all-to-all-start.2 = ((f32[2,2,16,128,128]{4,2,0,1,3:T(8,128)}), f32[2,2,16,128,128]{4,2,0,1,3:T(8,128)}, u32[]{:S(2)}, u32[]{:S(2)}) async-start(f32[2,2,16,128,128]{4,2,0,1,3:T(8,128)} %copy.157), calls=%async_computation.2 | async-start | bytes 8388608 | tf_op jit(solution)/shard_map/while/body/eval_jaxpr/all_to_all | solution.py:104
  153.5 2.2 copy-start.2
  197.4 8.0 copy-start.17
  197.4 97.3 %all-to-all-start.2 = ((f32[2,2,16,128,128]{4,2,0,1,3:T(8,128)}), f32[2,2,16,128,128]{4,2,0,1,3:T(8,128)}, u32[]{:S(2)}, u32[]{:S(2)}) async-start(f32[2,2,16,128,128]{4,2,0,1,3:T(8,128)} %copy.157), calls=%async_computation.2 | async-start | bytes 8388608 | tf_op jit(solution)/shard_map/while/body/eval_jaxpr/all_to_all | solution.py:104
  312.3 2.2 copy-start.2
  381.4 8.0 copy-start.18
  381.4 97.2 %all-to-all-start = ((f32[2,2,16,128,128]{4,2,0,1,3:T(8,128)}), f32[2,2,16,128,128]{4,2,0,1,3:T(8,128)}, u32[]{:S(2)}, u32[]{:S(2)}) async-start(f32[2,2,16,128,128]{4,2,0,1,3:T(8,128)} %copy.147), calls=%async_computation | async-start | bytes 8388608 | tf_op jit(solution)/shard_map/while/body/eval_jaxpr/all_to_all | solution.py:104
  496.2 2.2 copy-start.4
  543.4 8.0 copy-start.18
  543.4 97.2 %all-to-all-start = ((f32[2,2,16,128,128]{4,2,0,1,3:T(8,128)}), f32[2,2,16,128,128]{4,2,0,1,3:T(8,128)}, u32[]{:S(2)}, u32[]{:S(2)}) async-start(f32[2,2,16,128,128]{4,2,0,1,3:T(8,128)} %copy.147), calls=%async_computation | async-start | bytes 8388608 | tf_op jit(solution)/shard_map/while/body/eval_jaxpr/all_to_all | solution.py:104
  658.1 2.2 copy-start.4
  676.7 354.3 %copy-start.11 = (s32[16384]{0:T(1024)S(1)}, s32[16384]{0:T(1024)}, u32[]{:S(2)}) copy-start(s32[16384]{0:T(1024)} %fusion.346) | copy-start | bytes 196612
  727.8 8.0 copy-start.19
  727.8 97.2 %all-to-all-start.1 = ((f32[2,2,16,128,128]{4,2,0,1,3:T(8,128)}), f32[2,2,16,128,128]{4,2,0,1,3:T(8,128)}, u32[]{:S(2)}, u32[]{:S(2)}) async-start(f32[2,2,16,128,128]{4,2,0,1,3:T(8,128)} %copy.152), calls=%async_computation.1 | async-start | bytes 8388608 | tf_op jit(solution)/shard_map/while/body/eval_jaxpr/all_to_all | solution.py:104
  842.6 2.2 copy-start.6
  889.7 8.0 copy-start.19
  889.7 97.2 %all-to-all-start.1 = ((f32[2,2,16,128,128]{4,2,0,1,3:T(8,128)}), f32[2,2,16,128,128]{4,2,0,1,3:T(8,128)}, u32[]{:S(2)}, u32[]{:S(2)}) async-start(f32[2,2,16,128,128]{4,2,0,1,3:T(8,128)} %copy.152), calls=%async_computation.1 | async-start | bytes 8388608 | tf_op jit(solution)/shard_map/while/body/eval_jaxpr/all_to_all | solution.py:104
  1031.0 90.7 %copy-start.9 = (s32[16384]{0:T(1024)S(1)}, s32[16384]{0:T(1024)}, u32[]{:S(2)}) copy-start(s32[16384]{0:T(1024)} %param.16) | copy-start | bytes 196612
  1031.0 90.6 %copy-start.10 = (f32[16384]{0:T(1024)S(1)}, f32[16384]{0:T(1024)}, u32[]{:S(2)}) copy-start(f32[16384]{0:T(1024)} %get-tuple-element.865) | copy-start | bytes 196612
  1031.0 90.7 %copy-start.7 = (f32[3,16384]{1,0:T(4,128)S(1)}, f32[3,16384]{1,0:T(4,128)}, u32[]{:S(2)}) copy-start(f32[3,16384]{1,0:T(4,128)} %get-tuple-element.864) | copy-start | bytes 589828
  1031.0 90.7 %copy-start.8 = (f32[3,16384]{1,0:T(4,128)S(1)}, f32[3,16384]{1,0:T(4,128)}, u32[]{:S(2)}) copy-start(f32[3,16384]{1,0:T(4,128)} %get-tuple-element.866) | copy-start | bytes 589828
  1031.1 90.7 %copy-start.15 = (f32[3,3]{1,0:T(4,128)S(1)}, f32[3,3]{1,0:T(4,128)}, u32[]{:S(2)}) copy-start(f32[3,3]{1,0:T(4,128)} %fusion.349) | copy-start | bytes 112
  1031.1 91.2 %copy-start.12 = (f32[16384]{0:T(1024)S(1)}, f32[16384]{0:T(1024)}, u32[]{:S(2)}) copy-start(f32[16384]{0:T(1024)} %get-tuple-element.1115) | copy-start | bytes 196612
  1031.1 91.2 %copy-start.13 = (f32[16384]{0:T(1024)S(1)}, f32[16384]{0:T(1024)}, u32[]{:S(2)}) copy-start(f32[16384]{0:T(1024)} %get-tuple-element.1117) | copy-start | bytes 196612
  1031.1 91.2 %copy-start.14 = (f32[16384]{0:T(1024)S(1)}, f32[16384]{0:T(1024)}, u32[]{:S(2)}) copy-start(f32[16384]{0:T(1024)} %get-tuple-element.1116) | copy-start | bytes 196612
  1031.1 91.2 %copy-start.16 = (f32[16,32]{1,0:T(8,128)S(1)}, f32[16,32]{1,0:T(8,128)}, u32[]{:S(2)}) copy-start(f32[16,32]{1,0:T(8,128)} %custom-call.3) | copy-start | bytes 6148
  1031.1 91.2 %copy-start.20 = (f32[4]{0:T(128)S(1)}, f32[4]{0:T(128)}, u32[]{:S(2)}) copy-start(f32[4]{0:T(128)} %mul.627) | copy-start | bytes 52
  (9 other events, 18.8 us)
where the time goes:
time: 1360 us; the launch traced here: 1330 us
  waiting for transfers between devices  533 us (39%)
  matrix products  391 us (29%)
  local copies, waits for them, and re-layouts  237 us (17%)
  loops' own time  54.2 us (4%)
  starting transfers between devices  49.7 us (4%)
  blocking collectives  42.1 us (3%)
  other arithmetic  23.1 us (2%)
    all_to_all x6, waiting for transfers between devices, one_band(): lax.all_to_all(stacked, 'grid', split_axis=3, concat_axis=2, tiled=True)  533 us
    dot_general x16, matrix products, atom_block(): projected = jnp.dot(jnp.cos(phases), form_factor.T, precision=HIGHEST)  154 us
    gather x1, local copies, waits for them, and re-layouts, per_device(): selected = jnp.take(flat_spectrum, g_list)  90.5 us
    another operation x3, loops' own time, add_pairs(): return lax.fori_loop(0, block_bands, one_band, accumulated)  53.9 us
    dot_general x6, matrix products, one_band(): jnp.einsum('p,pxyz->xyz', weights, pair_power, precision=HIGHEST)  52 us
    all_to_all x6, starting transfers between devices, one_band(): lax.all_to_all(stacked, 'grid', split_axis=3, concat_axis=2, tiled=True)  46.3 us
    psum x1, blocking collectives, per_device(): stress, atom_terms = lax.psum((stress, atom_terms), ('band', 'grid'))  42.1 us
    another operation x6, local copies, waits for them, and re-layouts, one_band(): stacked = jnp.stack([real_y, imag_y], axis=1)  32.8 us
  transfers between devices with their start and end apart: 10, of which 6 were waited for; matrix products, arithmetic and copies ran while one was open for 20% of the time, Pallas kernels for 0%

commit v1 on v0

--- a/solution.py
+++ b/solution.py
@@ -101,7 +101,12 @@
             )
             stacked = jnp.stack([real_y, imag_y], axis=1)
             pair_power = finish_x(
-                lax.all_to_all(stacked, "grid", split_axis=3, concat_axis=2, tiled=True)
+                jnp.concatenate(
+                    lax.all_to_all(
+                        jnp.stack(jnp.split(stacked, lax.axis_size("grid"), axis=3)), "grid", 0, 0
+                    ),
+                    axis=2,
+                )
             )
             return running + jnp.einsum("p,pxyz->xyz", weights, pair_power, precision=HIGHEST)
 

time: 1360 us -> 1310 us (0.963)
  local copies, waits for them, and re-layouts: 237 us -> 191 us
  other arithmetic: 23.1 us -> 50.4 us
  matrix products: 391 us -> 375 us
    while x0 -> x42, other arithmetic: none -> 35.7 us
    another operation x6 -> x0, local copies, waits for them, and re-layouts: 32.8 us -> none  [one_band(): stacked = jnp.stack([real_y, imag_y], axis=1)]
    all_to_all x6 -> x0, local copies, waits for them, and re-layouts: 27.7 us -> none  [one_band(): lax.all_to_all(stacked, 'grid', split_axis=3, concat_axis=2, tiled=True)]
    reshape x0 -> x6, local copies, waits for them, and re-layouts: none -> 15.3 us  [one_band(): jnp.concatenate(lax.all_to_all(jnp.stack(jnp.split(stacked, lax.axis_size...]
  transfers between devices with their start and end apart: 10 -> 10, of which waited for: 6 -> 6; matrix products, arithmetic and copies ran while one was open for 20% -> 19% of each run, Pallas kernels for 0% -> 0%
where the time goes in v1:
time: 1310 us; the launch traced here: 1290 us
  waiting for transfers between devices  533 us (41%)
  matrix products  375 us (29%)
  local copies, waits for them, and re-layouts  191 us (15%)
  other arithmetic  50.4 us (4%)
  starting transfers between devices  49.7 us (4%)
  loops' own time  47.7 us (4%)
  blocking collectives  42.1 us (3%)
    all_to_all x6, waiting for transfers between devices, one_band(): lax.all_to_all(jnp.stack(jnp.split(stacked, lax.axis_size('grid'), axis=3...  533 us
    dot_general x16, matrix products, atom_block(): projected = jnp.dot(jnp.cos(phases), form_factor.T, precision=HIGHEST)  154 us
    gather x1, local copies, waits for them, and re-layouts, per_device(): selected = jnp.take(flat_spectrum, g_list)  90.5 us
    dot_general x6, matrix products, one_band(): jnp.einsum('p,pxyz->xyz', weights, pair_power, precision=HIGHEST)  52 us
    another operation x3, loops' own time, add_pairs(): return lax.fori_loop(0, block_bands, one_band, accumulated)  47.3 us
    all_to_all x6, starting transfers between devices, one_band(): lax.all_to_all(jnp.stack(jnp.split(stacked, lax.axis_size('grid'), axis=3...  46.3 us
    psum x1, blocking collectives, per_device(): stress, atom_terms = lax.psum((stress, atom_terms), ('band', 'grid'))  42.1 us
    while x42, other arithmetic  35.7 us
  transfers between devices with their start and end apart: 10, of which 6 were waited for; matrix products, arithmetic and copies ran while one was open for 19% of the time, Pallas kernels for 0%

profile of v1, /device:TPU:12, one launch (start us, length us, event | category | flops | bytes accessed | tf_op | source)
XLA Modules:
  0.0 1290.0 jit_solution(17536911958422384852)
XLA Ops:
  13.5 324.5 %while.62 = (s32[]{:T(128)}, f32[128,16,128]{2,1,0:T(8,128)S(1)}, f32[2]{0:T(128)}, f32[2,16,128,128]{3,2,1,0:T(8,128)}, s32[]{:T(128)}, /*index=5*/s32[]{:T(128)}) while((s32[]{:T(128)}, f32[128,16,128]{2,1,0:T(8,128)S(1)}, f32[2]{0:T(128)}, f32[2,16,128,128]{3,2,1,0:T(8,128)}, s32[]{:T(128)}, ...), condition=%wide.region_2.3_spmd.clone.clone, body=%wide.region_1.2_spmd.clone.clone.sunk | while | flops 8068988928 | bytes 167772464 | solution.py:113
  42.6 89.6 %all-to-all-done.2 = f32[8,2,2,16,16,128]{5,4,3,1,2,0:T(8,128)} async-done(((f32[8,2,2,16,16,128]{5,4,3,1,2,0:T(8,128)}), f32[8,2,2,16,16,128]{5,4,3,1,2,0:T(8,128)}, u32[]{:S(2)}, u32[]{:S(2)}) %all-to-all-start.2) | async-done | bytes 4194336 | tf_op jit(solution)/shard_map/while/body/eval_jaxpr/all_to_all | solution.py:105
  196.5 88.7 %all-to-all-done.2 = f32[8,2,2,16,16,128]{5,4,3,1,2,0:T(8,128)} async-done(((f32[8,2,2,16,16,128]{5,4,3,1,2,0:T(8,128)}), f32[8,2,2,16,16,128]{5,4,3,1,2,0:T(8,128)}, u32[]{:S(2)}, u32[]{:S(2)}) %all-to-all-start.2) | async-done | bytes 4194336 | tf_op jit(solution)/shard_map/while/body/eval_jaxpr/all_to_all | solution.py:105
  338.0 312.3 %while.60 = (s32[]{:T(128)}, f32[128,16,128]{2,1,0:T(8,128)S(1)}, f32[2]{0:T(128)}, f32[2]{0:T(128)}, f32[2,16,128,128]{3,2,1,0:T(8,128)}, /*index=5*/f32[2,16,128,128]{3,2,1,0:T(8,128)}, s32[]{:T(128)}) while((s32[]{:T(128)}, f32[128,16,128]{2,1,0:T(8,128)S(1)}, f32[2]{0:T(128)}, f32[2]{0:T(128)}, ...), condition=%wide.region_4.5_spmd.clone.clone, body=%wide.region_3.4_spmd.clone.clone.sunk | while | flops 8068726784 | bytes 159383824 | solution.py:113
  371.4 88.6 %all-to-all-done = f32[8,2,2,16,16,128]{5,4,3,1,2,0:T(8,128)} async-done(((f32[8,2,2,16,16,128]{5,4,3,1,2,0:T(8,128)}), f32[8,2,2,16,16,128]{5,4,3,1,2,0:T(8,128)}, u32[]{:S(2)}, u32[]{:S(2)}) %all-to-all-start) | async-done | bytes 4194336 | tf_op jit(solution)/shard_map/while/body/eval_jaxpr/all_to_all | solution.py:105
  485.0 8.9 fusion.593
  527.6 88.6 %all-to-all-done = f32[8,2,2,16,16,128]{5,4,3,1,2,0:T(8,128)} async-done(((f32[8,2,2,16,16,128]{5,4,3,1,2,0:T(8,128)}), f32[8,2,2,16,16,128]{5,4,3,1,2,0:T(8,128)}, u32[]{:S(2)}, u32[]{:S(2)}) %all-to-all-start) | async-done | bytes 4194336 | tf_op jit(solution)/shard_map/while/body/eval_jaxpr/all_to_all | solution.py:105
  641.2 8.9 fusion.593
  650.3 339.4 %while.61 = (s32[]{:T(128)}, f32[128,16,128]{2,1,0:T(8,128)S(1)}, f32[2]{0:T(128)}, f32[2]{0:T(128)}, f32[2,16,128,128]{3,2,1,0:T(8,128)}, /*index=5*/f32[2,16,128,128]{3,2,1,0:T(8,128)}, s32[]{:T(128)}) while((s32[]{:T(128)}, f32[128,16,128]{2,1,0:T(8,128)S(1)}, f32[2]{0:T(128)}, f32[2]{0:T(128)}, ...), condition=%wide.region_6.7_spmd.clone.clone, body=%wide.region_5.6_spmd.clone.clone.sunk | while | flops 8068726784 | bytes 159383824 | solution.py:113
  702.9 88.7 %all-to-all-done.1 = f32[8,2,2,16,16,128]{5,4,3,1,2,0:T(8,128)} async-done(((f32[8,2,2,16,16,128]{5,4,3,1,2,0:T(8,128)}), f32[8,2,2,16,16,128]{5,4,3,1,2,0:T(8,128)}, u32[]{:S(2)}, u32[]{:S(2)}) %all-to-all-start.1) | async-done | bytes 4194336 | tf_op jit(solution)/shard_map/while/body/eval_jaxpr/all_to_all | solution.py:105
  816.5 8.9 fusion.631
  859.1 88.7 %all-to-all-done.1 = f32[8,2,2,16,16,128]{5,4,3,1,2,0:T(8,128)} async-done(((f32[8,2,2,16,16,128]{5,4,3,1,2,0:T(8,128)}), f32[8,2,2,16,16,128]{5,4,3,1,2,0:T(8,128)}, u32[]{:S(2)}, u32[]{:S(2)}) %all-to-all-start.1) | async-done | bytes 4194336 | tf_op jit(solution)/shard_map/while/body/eval_jaxpr/all_to_all | solution.py:105
  972.7 8.9 fusion.631
  989.8 90.5 %gather_fusion = f32[16384]{0:T(1024)S(1)} fusion(f32[262144]{0:T(1024)S(1)} %bitcast.515, s32[16384]{0:T(1024)S(1)} %copy-done.11), kind=kCustom, calls=%fused_computation | custom fusion | bytes 196608 | tf_op jit(solution)/shard_map/jit(_take)/gather | solution.py:122
  1081.0 166.4 %while.59 = (s32[]{:T(128)}, f32[16,32]{1,0:T(8,128)S(1)}, f32[16,3,32]{2,0,1:T(8,128)}, f32[16384]{0:T(1024)S(1)}, f32[16384]{0:T(1024)S(1)}, /*index=5*/f32[16...) while((s32[]{:T(128)}, f32[16,32]{1,0:T(8,128)S(1)}, ...), condition=%wide.region_11.12_spmd.clone, body=%wide.region_9.11_spmd.clone.sunk | while | flops 28442852 | bytes 329921 | solution.py:60
  1081.7 9.6 fusion.555
  1092.1 9.6 fusion.555
  1102.5 9.6 fusion.555
  1112.9 9.6 fusion.555
  1123.3 9.6 fusion.555
  1133.7 9.6 fusion.555
  1144.1 9.6 fusion.555
  1154.5 9.7 fusion.555
  1164.9 9.6 fusion.555
  1175.3 9.7 fusion.555
  1185.7 9.6 fusion.555
  1196.1 9.7 fusion.555
  1206.6 9.6 fusion.555
  1217.0 9.6 fusion.555
  1227.3 9.6 fusion.555
  1237.7 9.6 fusion.555
  1247.5 42.1 %all-reduce = (f32[3,3]{1,0:T(4,128)}, f32[512]{0:T(512)}) all-reduce(f32[3,3]{1,0:T(4,128)S(1)} %broadcast_multiply_fusion.6, f32[512]{0:T(512)S(1)} %div.77), channel_id=1, replica_groups=mesh['band'=4,'grid'=8] {'band','grid'}, use_global_device_ids=true, to_apply=%region_8.9 | all-reduce | flops 521 | bytes 4168 | tf_op jit(solution)/shard_map/psum | solution.py:137
  (281 shorter events, 385.8 us)
Async XLA Ops:
  0.6 337.4 %collective-permute-start.1 = (f32[2,16,128,128]{3,2,1,0:T(8,128)}, f32[2,16,128,128]{3,2,1,0:T(8,128)}, u32[]{:S(2)}, u32[]{:S(2)}) collective-permute-start(f32[2,16,128,128]{3,2,1,0:T(8,128)} %param.14), channel_id=1, source_target_pairs={{0,8},{8,16},{16,24},{24,0},{1,9},{9,17},{17,25},{25,1},{2,10},{10... | collective-permute-start | bytes 6291464 | tf_op jit(solution)/shard_map/ppermute | solution.py:12
  0.7 649.6 %collective-permute-start.3 = (f32[2,16,128,128]{3,2,1,0:T(8,128)}, f32[2,16,128,128]{3,2,1,0:T(8,128)}, u32[]{:S(2)}, u32[]{:S(2)}) collective-permute-start(f32[2,16,128,128]{3,2,1,0:T(8,128)} %param.14), channel_id=1, source_target_pairs={{0,16},{8,24},{16,0},{24,8},{1,17},{9,25},{17,1},{25,9},{2,18},{10... | collective-permute-start | bytes 6291464 | tf_op jit(solution)/shard_map/ppermute | solution.py:12
  2.3 335.7 %collective-permute-start = (f32[2]{0:T(128)}, f32[2]{0:T(128)}, u32[]{:S(2)}, u32[]{:S(2)}) collective-permute-start(f32[2]{0:T(128)} %param.15), channel_id=1, source_target_pairs={{0,8},{8,16},{16,24},{24,0},{1,9},{9,17},{17,25},{25,1},{2,10},{10... | collective-permute-start | bytes 32 | tf_op jit(solution)/shard_map/ppermute | solution.py:12
  2.5 335.4 %collective-permute-start.2 = (f32[2]{0:T(128)}, f32[2]{0:T(128)}, u32[]{:S(2)}, u32[]{:S(2)}) collective-permute-start(f32[2]{0:T(128)} %param.15), channel_id=1, source_target_pairs={{0,16},{8,24},{16,0},{24,8},{1,17},{9,25},{17,1},{25,9},{2,18},{10... | collective-permute-start | bytes 32 | tf_op jit(solution)/shard_map/ppermute | solution.py:12
  35.7 6.4 copy-start.17
  35.7 96.5 %all-to-all-start.2 = ((f32[8,2,2,16,16,128]{5,4,3,1,2,0:T(8,128)}), f32[8,2,2,16,16,128]{5,4,3,1,2,0:T(8,128)}, u32[]{:S(2)}, u32[]{:S(2)}) async-start(f32[8,2,2,16,16,128]{5,4,3,1,2,0:T(8,128)} %fusion.664), calls=%async_computation.2 | async-start | bytes 8388608 | tf_op jit(solution)/shard_map/while/body/eval_jaxpr/all_to_all | solution.py:105
  147.7 2.2 copy-start.2
  187.9 8.0 copy-start.17
  187.9 97.3 %all-to-all-start.2 = ((f32[8,2,2,16,16,128]{5,4,3,1,2,0:T(8,128)}), f32[8,2,2,16,16,128]{5,4,3,1,2,0:T(8,128)}, u32[]{:S(2)}, u32[]{:S(2)}) async-start(f32[8,2,2,16,16,128]{5,4,3,1,2,0:T(8,128)} %fusion.664), calls=%async_computation.2 | async-start | bytes 8388608 | tf_op jit(solution)/shard_map/while/body/eval_jaxpr/all_to_all | solution.py:105
  362.8 8.0 copy-start.18
  362.8 97.2 %all-to-all-start = ((f32[8,2,2,16,16,128]{5,4,3,1,2,0:T(8,128)}), f32[8,2,2,16,16,128]{5,4,3,1,2,0:T(8,128)}, u32[]{:S(2)}, u32[]{:S(2)}) async-start(f32[8,2,2,16,16,128]{5,4,3,1,2,0:T(8,128)} %fusion.588), calls=%async_computation | async-start | bytes 8388608 | tf_op jit(solution)/shard_map/while/body/eval_jaxpr/all_to_all | solution.py:105
  475.6 2.2 copy-start.4
  519.0 8.0 copy-start.18
  519.0 97.2 %all-to-all-start = ((f32[8,2,2,16,16,128]{5,4,3,1,2,0:T(8,128)}), f32[8,2,2,16,16,128]{5,4,3,1,2,0:T(8,128)}, u32[]{:S(2)}, u32[]{:S(2)}) async-start(f32[8,2,2,16,16,128]{5,4,3,1,2,0:T(8,128)} %fusion.588), calls=%async_computation | async-start | bytes 8388608 | tf_op jit(solution)/shard_map/while/body/eval_jaxpr/all_to_all | solution.py:105
  631.7 2.2 copy-start.4
  650.3 339.4 %copy-start.11 = (s32[16384]{0:T(1024)S(1)}, s32[16384]{0:T(1024)}, u32[]{:S(2)}) copy-start(s32[16384]{0:T(1024)} %fusion.415) | copy-start | bytes 196612
  694.4 8.0 copy-start.19
  694.4 97.2 %all-to-all-start.1 = ((f32[8,2,2,16,16,128]{5,4,3,1,2,0:T(8,128)}), f32[8,2,2,16,16,128]{5,4,3,1,2,0:T(8,128)}, u32[]{:S(2)}, u32[]{:S(2)}) async-start(f32[8,2,2,16,16,128]{5,4,3,1,2,0:T(8,128)} %fusion.626), calls=%async_computation.1 | async-start | bytes 8388608 | tf_op jit(solution)/shard_map/while/body/eval_jaxpr/all_to_all | solution.py:105
  807.1 2.2 copy-start.6
  850.5 8.0 copy-start.19
  850.5 97.2 %all-to-all-start.1 = ((f32[8,2,2,16,16,128]{5,4,3,1,2,0:T(8,128)}), f32[8,2,2,16,16,128]{5,4,3,1,2,0:T(8,128)}, u32[]{:S(2)}, u32[]{:S(2)}) async-start(f32[8,2,2,16,16,128]{5,4,3,1,2,0:T(8,128)} %fusion.626), calls=%async_computation.1 | async-start | bytes 8388608 | tf_op jit(solution)/shard_map/while/body/eval_jaxpr/all_to_all | solution.py:105
  963.2 2.2 copy-start.6
  989.7 90.7 %copy-start.9 = (s32[16384]{0:T(1024)S(1)}, s32[16384]{0:T(1024)}, u32[]{:S(2)}) copy-start(s32[16384]{0:T(1024)} %param.16) | copy-start | bytes 196612
  989.7 90.6 %copy-start.10 = (f32[16384]{0:T(1024)S(1)}, f32[16384]{0:T(1024)}, u32[]{:S(2)}) copy-start(f32[16384]{0:T(1024)} %get-tuple-element.855) | copy-start | bytes 196612
  989.7 90.7 %copy-start.7 = (f32[3,16384]{1,0:T(4,128)S(1)}, f32[3,16384]{1,0:T(4,128)}, u32[]{:S(2)}) copy-start(f32[3,16384]{1,0:T(4,128)} %get-tuple-element.854) | copy-start | bytes 589828
  989.7 90.7 %copy-start.8 = (f32[3,16384]{1,0:T(4,128)S(1)}, f32[3,16384]{1,0:T(4,128)}, u32[]{:S(2)}) copy-start(f32[3,16384]{1,0:T(4,128)} %get-tuple-element.856) | copy-start | bytes 589828
  989.7 90.7 %copy-start.15 = (f32[3,3]{1,0:T(4,128)S(1)}, f32[3,3]{1,0:T(4,128)}, u32[]{:S(2)}) copy-start(f32[3,3]{1,0:T(4,128)} %fusion.418) | copy-start | bytes 112
  989.8 91.2 %copy-start.12 = (f32[16384]{0:T(1024)S(1)}, f32[16384]{0:T(1024)}, u32[]{:S(2)}) copy-start(f32[16384]{0:T(1024)} %get-tuple-element.1105) | copy-start | bytes 196612
  989.8 91.2 %copy-start.13 = (f32[16384]{0:T(1024)S(1)}, f32[16384]{0:T(1024)}, u32[]{:S(2)}) copy-start(f32[16384]{0:T(1024)} %get-tuple-element.1107) | copy-start | bytes 196612
  989.8 91.2 %copy-start.14 = (f32[16384]{0:T(1024)S(1)}, f32[16384]{0:T(1024)}, u32[]{:S(2)}) copy-start(f32[16384]{0:T(1024)} %get-tuple-element.1106) | copy-start | bytes 196612
  989.8 91.2 %copy-start.16 = (f32[16,32]{1,0:T(8,128)S(1)}, f32[16,32]{1,0:T(8,128)}, u32[]{:S(2)}) copy-start(f32[16,32]{1,0:T(8,128)} %custom-call.6) | copy-start | bytes 6148
  989.8 91.2 %copy-start.20 = (f32[4]{0:T(128)S(1)}, f32[4]{0:T(128)}, u32[]{:S(2)}) copy-start(f32[4]{0:T(128)} %mul.627) | copy-start | bytes 52
  (9 other events, 18.8 us)
